TPU v7x, 32 devices: a whole 2x2x4 slice. The times are simulated.
32 devices in a mesh: mod: 2 (over y), dp: 16 (over z, x, core).
Axes of the slice: x: 2, y: 2, z: 4, core: 2. Of those that a mesh axis runs over, the one named last changes fastest.
Arguments:
- image_pooled: bfloat16 [640, 1024], P('dp'), may hold values from -6 to 6
- text_pooled: bfloat16 [640, 768], P('dp'), may hold values from -6 to 6
- image_gain: float32 [1024], replicated, may hold values from 0.25 to 1.75
- text_gain: float32 [768], replicated, may hold values from 0.25 to 1.75
- image_proj: bfloat16 [1024, 768], replicated, may hold values from -0.1875 to 0.1875
- text_proj: bfloat16 [768, 768], replicated, may hold values from -0.21875 to 0.21875
- logit_scale: float32 [1], replicated, may hold values from 10 to 100
- pair_index: int32 [2, 640], P('mod', 'dp'), may hold values from 0 to 639, as said below
Outputs:
- loss_value: float32 [], replicated
- embed_grad: float32 [2, 640, 768], P('mod', 'dp')
Inputs may be any that keep to these rules, and one draw needn't show every extreme that they name: `pair_index`: row 0 is a permutation of 0 to 639 and row 1 is its inverse permutation.
All inputs are finite; a program needn't handle non-finite values.
Results may differ from a plain program's by a relative error of at most 0.0041.
Values may be sent and summed in bfloat16 or wider, within the bound.
A program may use at most 128 MiB of HBM per device.

v0:
```python
import jax
import jax.numpy as jnp
from jax import lax
from jax.sharding import PartitionSpec as P


def from_partner(x, axis, bit):
    return lax.ppermute(x, axis, [(i, i ^ 1 << bit) for i in range(lax.axis_size(axis))])


def normalize_project(pooled, gain, weight):
    features = pooled.astype(jnp.float32)
    centered = features - jnp.mean(features, axis=-1, keepdims=True)
    variance = jnp.mean(centered * centered, axis=-1, keepdims=True)
    normalized = (centered * lax.rsqrt(variance + 1e-05) * gain).astype(jnp.bfloat16)
    return jnp.dot(normalized, weight, preferred_element_type=jnp.float32)


def unitize(embedded):
    lengths = jnp.sqrt(jnp.sum(embedded * embedded, axis=-1, keepdims=True) + 1e-06)
    return (embedded / lengths, lengths)


def similarity(left_rows, right_rows, scale_value):
    return scale_value * lax.dot_general(
        left_rows, right_rows, (((1,), (1,)), ((), ())), preferred_element_type=jnp.float32
    )


def local(
    image_pooled, text_pooled, image_gain, text_gain, image_proj, text_proj, logit_scale, pair_index
):
    module_index = lax.axis_index("mod")
    embedded = lax.cond(
        module_index == 0,
        lambda: normalize_project(image_pooled, image_gain, image_proj),
        lambda: normalize_project(text_pooled, text_gain, text_proj),
    )
    unit_rows, lengths = unitize(embedded)
    unit_half = unit_rows.astype(jnp.bfloat16)
    mirror_rows = from_partner(unit_half, "mod", 0)
    scale_value = logit_scale[0]
    row_count = unit_rows.shape[0]
    batch_total = row_count * lax.axis_size("dp")
    gathered = lax.all_gather(mirror_rows, "dp", axis=0, tiled=True)
    scores = similarity(unit_half, gathered, scale_value)
    running_max = jnp.max(scores, axis=1)
    own_lse = running_max + jnp.log(jnp.sum(jnp.exp(scores - running_max[:, None]), axis=1))
    columns = lax.broadcasted_iota(jnp.int32, (row_count, batch_total), 1)
    matched = columns == pair_index[0][:, None]
    diagonal = jnp.sum(jnp.where(matched, scores, 0.0), axis=1)
    every_lse, every_diag = (
        lax.all_gather(own_lse, ("mod", "dp"), axis=0, tiled=True),
        lax.all_gather(diagonal, ("mod", "dp"), axis=0, tiled=True),
    )
    other_lse = lax.dynamic_slice_in_dim(every_lse, (1 - module_index) * batch_total, batch_total)
    loss_value = (jnp.sum(every_lse) - jnp.sum(every_diag)) / (2.0 * batch_total)
    pair_weight = (
        jnp.exp(scores - own_lse[:, None])
        + jnp.exp(scores - other_lse[None, :])
        - 2.0 * matched.astype(jnp.float32)
    ).astype(jnp.bfloat16)
    unit_grad = (
        scale_value
        / (2.0 * batch_total)
        * jnp.dot(pair_weight, gathered, preferred_element_type=jnp.float32)
    )
    embed_grad = (
        unit_grad - unit_rows * jnp.sum(unit_rows * unit_grad, axis=-1, keepdims=True)
    ) / lengths
    return (loss_value, embed_grad[None])


def solution(mesh):
    in_specs = (P("dp", None), P("dp", None), P(), P(), P(), P(), P(), P("mod", "dp"))
    out_specs = (P(), P("mod", "dp", None))
    return jax.shard_map(local, mesh=mesh, in_specs=in_specs, out_specs=out_specs, check_vma=False)
```

profile of v0, /device:TPU:0, one launch (start us, length us, event | category | flops | bytes accessed | tf_op | source)
XLA Modules:
  0.0 78.1 jit_solution(6129029324738736359)
XLA Ops:
  0.6 4.1 %conditional.1 = (f32[40,768]{1,0:T(8,128)S(1)}, f32[40,1]{0,1:T(1,128)S(1)}) conditional(s32[]{:T(128)} %convert_element_type.22, (bf16[40,768]{1,0:T(8,128)(2,1)}, f32[768]{0:T(1024)}, bf16[768,768]{1,0:T(8,128)(2,1)}) %tuple.18, (bf16[40,1024]{1,0:T(8,128)(2,1)}, f32[1024]{0:T(1024)}, bf16[1024,768]{1,0:T(8,128)(2,1)}) %tuple.19), branch_computations={%region_0.4_spmd, %region_4.8_spmd} | conditional | flops 63426560 | bytes 1947216 | solution.py:34
  0.7 1.0 %convert_reduce_fusion.1 = f32[40]{0:T(128)S(1)} fusion(bf16[40,1024]{1,0:T(8,128)(2,1)} %get-tuple-element.35), kind=kLoop, calls=%fused_computation.15 | loop fusion | flops 81880 | bytes 82080 | tf_op jit(solution)/shard_map/cond/branch_1_fun/reduce_sum | solution.py:13
  1.7 1.1 %fusion.12 = f32[40]{0:T(128)S(1)} fusion(bf16[40,1024]{1,0:T(8,128)(2,1)} %get-tuple-element.35, f32[40]{0:T(128)S(1)} %broadcast_multiply_fusion.1), kind=kLoop, calls=%fused_computation.18 | loop fusion | flops 163800 | bytes 82240 | tf_op jit(solution)/shard_map/cond/branch_1_fun/reduce_sum | solution.py:14
  2.8 2.0 %multiply_reduce_fusion.1 = (f32[40]{0:T(128)S(1)}, f32[40,768]{1,0:T(8,128)S(1)}) fusion(bf16[1024,768]{1,0:T(8,128)(2,1)} %get-tuple-element.37, bf16[40,1024]{1,0:T(8,128)(2,1)} %get-tuple-element.35, f32[1024]{0:T(1024)} %get-tuple-element.36, f32[40]{0:T(128)S(1)} %add_rsqrt_fusion.1, f32[40]{0:T(128)S(1)} %broadcast_multiply_fusion.1), kind=kOutput, calls=%fused_computation.21 | convolution fusion | flops 63180760 | bytes 1782240 | tf_op jit(solution)/shard_map/cond/branch_1_fun/dot_general | solution.py:16
  4.8 0.0 copy-start
  4.8 0.1 fusion.27
  4.9 2.7 %collective-permute-start = (bf16[40,768]{1,0:T(8,128)(2,1)S(1)}, bf16[40,768]{1,0:T(8,128)(2,1)S(1)}, u32[]{:S(2)}, u32[]{:S(2)}) collective-permute-start(bf16[40,768]{1,0:T(8,128)(2,1)S(1)} %fusion.27), channel_id=1, source_target_pairs={{0,16},{16,0},{1,17},{17,1},{2,18},{18,2},{3,19},{19,3},{4,20},{20... | collective-permute-start | bytes 184328 | tf_op jit(solution)/shard_map/ppermute | solution.py:8
  8.3 1.5 %collective-permute-done = bf16[40,768]{1,0:T(8,128)(2,1)S(1)} collective-permute-done((bf16[40,768]{1,0:T(8,128)(2,1)S(1)}, bf16[40,768]{1,0:T(8,128)(2,1)S(1)}, u32[]{:S(2)}, u32[]{:S(2)}) %collective-permute-start) | collective-permute-done | bytes 61472 | tf_op jit(solution)/shard_map/ppermute | solution.py:8
  9.8 25.3 %all_gather.9 = bf16[640,768]{1,0:T(8,128)(2,1)S(1)} all-gather(bf16[40,768]{1,0:T(8,128)(2,1)S(1)} %collective-permute-done), channel_id=1, replica_groups=mesh['mod'=2,'dp'=16] {'dp'}, dimensions={0}, use_global_device_ids=true | all-gather | bytes 1044480 | tf_op jit(solution)/shard_map/all_gather | solution.py:45
  35.1 0.5 fusion.29
  35.6 0.0 copy-done
  35.6 0.2 select_reduce_fusion
  35.8 0.3 dynamic-update-slice.1
  36.1 0.1 fusion.28
  36.2 37.0 %all-reduce.2 = (f32[1280]{0:T(1024)S(1)}, f32[1280]{0:T(1024)S(1)}) all-reduce(f32[1280]{0:T(1024)S(1)} %get-tuple-element.42, f32[1280]{0:T(1024)S(1)} %dynamic-update-slice.1), channel_id=1, replica_groups=mesh['mod'=2,'dp'=16] {'mod','dp'}, use_global_device_ids=true, to_apply=%add | all-reduce | flops 2560 | bytes 20480
  73.2 0.6 reduce_sum.102
  73.8 0.6 reduce_sum.104
  75.7 0.1 dynamic_slice.3
  75.8 0.4 multiply_reduce_fusion.2
  76.2 0.8 divide_bitcast_fusion
  (5 shorter events, 0.0 us)
Async XLA Ops:
  4.8 30.9 %copy-start = (s32[1,40]{1,0:T(1,128)S(1)}, s32[1,40]{1,0:T(1,128)}, u32[]{:S(2)}) copy-start(s32[1,40]{1,0:T(1,128)} %param.17) | copy-start | bytes 484
  4.9 4.9 %collective-permute-start = (bf16[40,768]{1,0:T(8,128)(2,1)S(1)}, bf16[40,768]{1,0:T(8,128)(2,1)S(1)}, u32[]{:S(2)}, u32[]{:S(2)}) collective-permute-start(bf16[40,768]{1,0:T(8,128)(2,1)S(1)} %fusion.27), channel_id=1, source_target_pairs={{0,16},{16,0},{1,17},{17,1},{2,18},{18,2},{3,19},{19,3},{4,20},{20... | collective-permute-start | bytes 184328 | tf_op jit(solution)/shard_map/ppermute | solution.py:8
where the time goes:
time: 79 us; the launch traced here: 78.1 us
  blocking collectives  62.3 us (79%)
  other arithmetic  4.46 us (6%)
  between operations  3.76 us (5%)
  matrix products  2.94 us (4%)
  starting transfers between devices  2.74 us (3%)
  waiting for transfers between devices  1.55 us (2%)
    unnamed x1, blocking collectives  37 us
    all_gather x1, blocking collectives, local(): gathered = lax.all_gather(mirror_rows, 'dp', axis=0, tiled=True)  25.3 us
    ppermute x1, starting transfers between devices, from_partner(): lax.ppermute(x, axis, [(i, i ^ 1 << bit) for i in range(lax.axis_size(axi...  2.74 us
    dot_general x1, matrix products, normalize_project(): return jnp.dot(normalized, weight, preferred_element_type=jnp.float32)  2 us
  transfers between devices with their start and end apart: 1, of which 1 were waited for; matrix products, arithmetic and copies ran while one was open for 0% of the time, Pallas kernels for 0%

commit v1 on v0

v1 whole, which is shorter than its diff:
```python
import functools

import jax
import jax.numpy as jnp
from jax import lax
from jax.experimental import pallas as pl
from jax.experimental.pallas import tpu as pltpu
from jax.sharding import PartitionSpec as P

MESH = pl.DeviceIdType.MESH
UNROLL = 32


def loop(count, body):
    if count <= UNROLL:
        for step in range(count):
            body(step)
    else:
        pl.loop(0, count)(body)


def fold(count, body, init):
    if count <= UNROLL:
        for step in range(count):
            init = body(step, init)
        return init
    return lax.fori_loop(0, count, body, init)


def kernel(
    n_mod, n_dp,
    image_ref, text_ref, image_gain_ref, text_gain_ref, image_proj_ref, text_proj_ref, scale_ref, pair_ref,
    loss_ref, grad_ref,
    image_w, text_w, rows_all, unit, length, scores, base, note, notes,
    w_sem, send_sem, recv_sem, note_send, note_recv,
):
    module, me = lax.axis_index("mod"), lax.axis_index("dp")
    n_all = n_mod * n_dp
    n_line = n_dp // 4
    line, side, core = me // 4, (me // 2) % 2, me % 2
    here = module * n_dp + me
    row_count = image_ref.shape[0]
    across = (line * 2 + (1 - side)) * 2 + core
    twin = me + 1 - 2 * core

    image_copy = pltpu.make_async_copy(image_proj_ref, image_w, w_sem.at[0])
    text_copy = pltpu.make_async_copy(text_proj_ref, text_w, w_sem.at[1])

    @pl.when(module == 0)
    def _():
        text_copy.start()
        image_copy.start()

    @pl.when(module != 0)
    def _():
        image_copy.start()
        text_copy.start()

    barrier = pltpu.get_barrier_semaphore()

    def greet(step):
        other = (here + step + 1) % n_all
        pl.semaphore_signal(
            barrier, inc=1, device_id=(other // n_dp, other % n_dp), device_id_type=MESH
        )

    loop(n_all - 1, greet)

    def embed(pooled_ref, gain_ref, copy, w):
        features = pooled_ref[...].astype(jnp.float32)
        centered = features - jnp.mean(features, axis=-1, keepdims=True)
        variance = jnp.mean(centered * centered, axis=-1, keepdims=True)
        normed = centered * lax.rsqrt(variance + 1e-05) * gain_ref[...].reshape(1, -1)
        normed = normed.astype(jnp.bfloat16)
        copy.wait()
        embedded = jnp.dot(normed, w[...], preferred_element_type=jnp.float32)
        lengths = jnp.sqrt(jnp.sum(embedded * embedded, axis=-1, keepdims=True) + 1e-06)
        return embedded / lengths, lengths

    def embed_other(*args):
        rows, _ = embed(*args)
        rows_all[me] = rows.astype(jnp.bfloat16)

    def embed_own(*args):
        unit[...], length[...] = embed(*args)

    image_args = (image_ref, image_gain_ref, image_copy, image_w)
    text_args = (text_ref, text_gain_ref, text_copy, text_w)

    pl.when(module == 0)(lambda: embed_other(*text_args))
    pl.when(module != 0)(lambda: embed_other(*image_args))

    pl.semaphore_wait(barrier, n_all - 1)

    def send(block, target, sem):
        return pltpu.make_async_remote_copy(
            src_ref=rows_all.at[block], dst_ref=rows_all.at[block],
            send_sem=send_sem.at[sem], recv_sem=recv_sem.at[block],
            device_id=(module, target), device_id_type=MESH,
        )

    def on_line(step):
        return (line + step) % n_line

    def peer(step, b, c):
        return (on_line(step) * 2 + b) * 2 + c

    def line_send(step):
        return send(me, peer(step, side, core), step)

    def across_send(step):
        return send(peer(step, side, core), across, n_line + step)

    def twin_send(step, b):
        return send(peer(step, b, core), twin, n_line * (2 + (b + side) % 2) + step)

    across_send(0).start()
    loop(n_line - 1, lambda step: line_send(step + 1).start())
    twin_send(0, side).start()

    pl.when(module == 0)(lambda: embed_own(*image_args))
    pl.when(module != 0)(lambda: embed_own(*text_args))
    own_half = unit[...].astype(jnp.bfloat16)
    scale_value = scale_ref[0]

    def score(block):
        scores[block] = scale_value * lax.dot_general(
            own_half, rows_all[block], (((1,), (1,)), ((), ())), preferred_element_type=jnp.float32
        )

    def arrive(block):
        send(block, twin, 0).wait_recv()

    score(me)

    def from_line(step):
        block = peer(step + 1, side, core)
        arrive(block)
        across_send(step + 1).start()
        twin_send(step + 1, side).start()
        score(block)

    def from_across(step):
        block = peer(step, 1 - side, core)
        arrive(block)
        twin_send(step, 1 - side).start()
        score(block)

    def from_twin(b, step):
        block = peer(step, b, 1 - core)
        arrive(block)
        score(block)

    loop(n_line - 1, from_line)
    loop(n_line, from_across)
    loop(n_line, functools.partial(from_twin, side))
    loop(n_line, functools.partial(from_twin, 1 - side))

    square = (row_count, row_count)
    down = lax.broadcasted_iota(jnp.int32, square, 0)
    over = lax.broadcasted_iota(jnp.int32, square, 1)
    pairs = jnp.sum(
        jnp.where(down == over, pair_ref[...].astype(jnp.float32), 0.0), axis=1, keepdims=True
    ).astype(jnp.int32)

    def matched(block):
        return over + block * row_count == pairs

    peak = fold(n_dp, lambda p, acc: jnp.maximum(acc, scores[p]), jnp.full(square, -jnp.inf, jnp.float32))
    peak = jnp.max(peak, axis=1, keepdims=True)

    def gather_sums(p, acc):
        total, diagonal = acc
        block = scores[p]
        return total + jnp.exp(block - peak), diagonal + jnp.where(matched(p), block, 0.0)

    zero = jnp.zeros(square, jnp.float32)
    total, diagonal = fold(n_dp, gather_sums, (zero, zero))
    lse = peak + jnp.log(jnp.sum(total, axis=1, keepdims=True))
    excess = lse - jnp.sum(diagonal, axis=1, keepdims=True)

    lanes = note.shape[-1]
    wide = (row_count, lanes)
    lane = lax.broadcasted_iota(jnp.int32, wide, 1)
    placed = jnp.where(
        lane == lax.broadcasted_iota(jnp.int32, wide, 0), lse, jnp.where(lane == lanes - 1, excess, 0.0)
    )
    note[...] = jnp.sum(placed, axis=0, keepdims=True)
    notes[here] = note[...]

    def note_copy(step):
        other = (here + step + 1) % n_all
        return pltpu.make_async_remote_copy(
            src_ref=note, dst_ref=notes.at[here],
            send_sem=note_send.at[step], recv_sem=note_recv.at[here],
            device_id=(other // n_dp, other % n_dp), device_id_type=MESH,
        )

    loop(n_all - 1, lambda step: note_copy(step).start())

    def first_half(p):
        base[p] = jnp.exp(scores[p] - lse) - jnp.where(matched(p), 2.0, 0.0)

    loop(n_dp, first_half)

    def note_arrive(step):
        other = (here + step + 1) % n_all
        pltpu.make_async_remote_copy(
            src_ref=note, dst_ref=notes.at[other],
            send_sem=note_send.at[step], recv_sem=note_recv.at[other],
            device_id=(other // n_dp, other % n_dp), device_id_type=MESH,
        ).wait_recv()

    loop(n_all - 1, note_arrive)

    loss = fold(n_all, lambda p, acc: acc + notes[p], jnp.zeros((1, lanes), jnp.float32))
    loss_ref[...] = loss[:, lanes - 1 :] / (2.0 * n_dp * row_count)

    def weigh(p, acc):
        other = notes[(1 - module) * n_dp + p][:, :row_count]
        weight = (base[p] + jnp.exp(scores[p] - other)).astype(jnp.bfloat16)
        return acc + jnp.dot(weight, rows_all[p], preferred_element_type=jnp.float32)

    moved = fold(n_dp, weigh, jnp.zeros(grad_ref.shape[1:], jnp.float32))
    moved = scale_value / (2.0 * n_dp * row_count) * moved
    own = unit[...]
    grad_ref[0] = (moved - own * jnp.sum(own * moved, axis=-1, keepdims=True)) / length[...]

    loop(n_line - 1, lambda step: line_send(step + 1).wait_send())
    loop(n_line, lambda step: across_send(step).wait_send())
    loop(n_line, lambda step: twin_send(step, side).wait_send())
    loop(n_line, lambda step: twin_send(step, 1 - side).wait_send())
    loop(n_all - 1, lambda step: note_copy(step).wait_send())


def solution(mesh):
    n_mod, n_dp = mesh.shape["mod"], mesh.shape["dp"]

    def local(
        image_pooled, text_pooled, image_gain, text_gain, image_proj, text_proj, logit_scale, pair_index
    ):
        rows = image_pooled.shape[0]
        width = image_proj.shape[1]
        lanes = -(-(rows + 1) // 128) * 128
        n_all = n_mod * n_dp
        vmem = pl.BlockSpec(memory_space=pltpu.VMEM)
        anywhere = pl.BlockSpec(memory_space=pl.ANY)
        dma = pltpu.SemaphoreType.DMA
        loss, grad = pl.pallas_call(
            functools.partial(kernel, n_mod, n_dp),
            out_shape=(
                jax.ShapeDtypeStruct((1, 1), jnp.float32),
                jax.ShapeDtypeStruct((1, rows, width), jnp.float32),
            ),
            in_specs=[vmem] * 4 + [anywhere] * 2 + [pl.BlockSpec(memory_space=pltpu.SMEM), vmem],
            out_specs=(vmem, vmem),
            scratch_shapes=[
                pltpu.VMEM(image_proj.shape, image_proj.dtype),
                pltpu.VMEM(text_proj.shape, text_proj.dtype),
                pltpu.VMEM((n_dp, rows, width), jnp.bfloat16),
                pltpu.VMEM((rows, width), jnp.float32),
                pltpu.VMEM((rows, 1), jnp.float32),
                pltpu.VMEM((n_dp, rows, rows), jnp.float32),
                pltpu.VMEM((n_dp, rows, rows), jnp.float32),
                pltpu.VMEM((1, lanes), jnp.float32),
                pltpu.VMEM((n_all, 1, lanes), jnp.float32),
                dma((2,)),
                dma((n_dp,)),
                dma((n_dp,)),
                dma((n_all,)),
                dma((n_all,)),
            ],
            compiler_params=pltpu.CompilerParams(collective_id=0, has_side_effects=True),
        )(image_pooled, text_pooled, image_gain, text_gain, image_proj, text_proj, logit_scale, pair_index)
        return loss[0, 0], grad

    in_specs = (P("dp", None), P("dp", None), P(), P(), P(), P(), P(), P("mod", "dp"))
    out_specs = (P(), P("mod", "dp", None))
    return jax.shard_map(local, mesh=mesh, in_specs=in_specs, out_specs=out_specs, check_vma=False)
```

time: 79 us -> 33.1 us (0.42)
  blocking collectives: 62.3 us -> 0 us
  Pallas kernels: 0 us -> 28.2 us
  other arithmetic: 4.46 us -> 0 us
  matrix products: 2.94 us -> 0 us
  starting transfers between devices: 2.74 us -> 0 us
  waiting for transfers between devices: 1.55 us -> 0 us
  local copies, waits for them, and re-layouts: 0.37 us -> 1.56 us
    unnamed x1 -> x0, blocking collectives: 37 us -> none
    pallas_call x0 -> x1, Pallas kernels: none -> 28.2 us  [local(): pl.pallas_call(functools.partial(kernel, n_mod, n_dp), out_shape=(jax.Sha...]
    all_gather x1 -> x0, blocking collectives: 25.3 us -> none  [local(): gathered = lax.all_gather(mirror_rows, 'dp', axis=0, tiled=True)]
    reduce_sum x5 -> x0, other arithmetic: 3.49 us -> none  [the longest x1 1.08 us: normalize_project(): variance = jnp.mean(centered * centered, axis=-1, keepdims=True)]
    dot_general x3 -> x0, matrix products: 2.94 us -> none  [the longest x1 2 us: normalize_project(): return jnp.dot(normalized, weight, preferred_element_type=jnp.float32)]
    ppermute x1 -> x0, starting transfers between devices: 2.74 us -> none  [from_partner(): lax.ppermute(x, axis, [(i, i ^ 1 << bit) for i in range(lax.axis_size(axi...]
    ppermute x1 -> x0, waiting for transfers between devices: 1.55 us -> none  [from_partner(): lax.ppermute(x, axis, [(i, i ^ 1 << bit) for i in range(lax.axis_size(axi...]
    unnamed x5 -> x1, local copies, waits for them, and re-layouts: 0.29 us -> 1.56 us
  transfers between devices with their start and end apart: 1 -> 0, of which waited for: 1 -> 0; matrix products, arithmetic and copies ran while one was open for 0% -> 0% of each run, Pallas kernels for 0% -> 0%
where the time goes in v1:
time: 33.1 us; the launch traced here: 32.9 us
  Pallas kernels  28.2 us (85%)
  between operations  3.1 us (9%)
  local copies, waits for them, and re-layouts  1.56 us (5%)
    pallas_call x1, Pallas kernels, local(): pl.pallas_call(functools.partial(kernel, n_mod, n_dp), out_shape=(jax.Sha...  28.2 us
    unnamed x1, local copies, waits for them, and re-layouts  1.56 us

profile of v1, /device:TPU:0, one launch (start us, length us, event | category | flops | bytes accessed | tf_op | source)
XLA Modules:
  0.0 32.9 jit_solution(10084264295021002793)
XLA Ops:
  1.3 28.2 %shard_map.95 = (f32[1,1]{1,0:T(1,128)}, f32[1,40,768]{2,1,0:T(8,128)}) custom-call(bf16[40,1024]{1,0:T(8,128)(2,1)} %image_ref.1, bf16[40,768]{1,0:T(8,128)(2,1)} %text_ref.1, f32[1024]{0:T(1024)} %image_gain_ref.1, f32[768]{0:T(1024)} %text_gain_ref.1, bf16[1024,768]{1,0:T(8,128)(2,1)} %image_proj_ref.1, bf16[768,768]{1,0:T(8,128)(2,1)} %text_proj_ref.1, ...), custom_call_target="tpu_custom_call" | custom-call | tf_op jit(solution)/shard_map/pallas_call | solution.py:249
  30.2 1.6 %copy.14 = f32[1,40,768]{2,1,0:T(8,128)} copy(f32[1,40,768]{2,1,0:T(8,128)} %get-tuple-element.9) | data formatting | bytes 245760

commit v2 on v1

v2 whole, which is shorter than its diff:
```python
import functools

import jax
import jax.numpy as jnp
from jax import lax
from jax.experimental import pallas as pl
from jax.experimental.pallas import tpu as pltpu
from jax.sharding import PartitionSpec as P

MESH = pl.DeviceIdType.MESH
UNROLL = 32
CHUNKS = 2


def pick(index, values):
    chosen = 0
    for at, value in enumerate(values):
        chosen = chosen + jnp.where(index == at, value, 0)
    return chosen


def by_distance(index, count, step, far):
    if count > 8:
        return (index + 1 + step) % count
    tables = [
        sorted((p for p in range(count) if p != i), key=lambda p: -abs(p - i) if far else abs(p - i))[step]
        for i in range(count)
    ]
    return pick(index, tables)


def loop(count, body):
    if count <= UNROLL:
        for step in range(count):
            body(step)
    else:
        pl.loop(0, count)(body)


def fold(count, body, init):
    if count <= UNROLL:
        for step in range(count):
            init = body(step, init)
        return init
    return lax.fori_loop(0, count, body, init)


def kernel(
    n_mod, n_dp,
    image_hbm, text_hbm, image_gain_hbm, text_gain_hbm, image_proj_ref, text_proj_ref, scale_hbm, pair_hbm,
    loss_ref, grad_ref,
    image_ref, text_ref, image_gain_ref, text_gain_ref, scale_ref, pair_ref,
    image_w, text_w, rows_all, unit, length, scores, base, note, notes,
    in_sem, w_sem, send_sem, recv_sem, note_send, note_recv, ready,
):
    module, me = lax.axis_index("mod"), lax.axis_index("dp")
    n_all = n_mod * n_dp
    n_line = n_dp // 4
    line, side, core = me // 4, (me // 2) % 2, me % 2
    here = module * n_dp + me
    row_count = image_ref.shape[0]
    across = (line * 2 + (1 - side)) * 2 + core
    twin = me + 1 - 2 * core
    mirror = 1 - module

    def peer(q, b, c):
        return (q * 2 + b) * 2 + c

    barrier = pltpu.get_barrier_semaphore()

    def greet(target_module, target):
        pl.semaphore_signal(barrier, inc=1, device_id=(target_module, target), device_id_type=MESH)

    loop(n_line - 1, lambda step: greet(module, peer((line + step + 1) % n_line, side, core)))
    greet(module, across)
    greet(module, twin)
    greet(mirror, me)

    image_copy = pltpu.make_async_copy(image_proj_ref, image_w, w_sem.at[0])
    text_copy = pltpu.make_async_copy(text_proj_ref, text_w, w_sem.at[1])
    small = [
        pltpu.make_async_copy(source, target, in_sem.at[at])
        for at, (source, target) in enumerate([
            (image_hbm, image_ref), (text_hbm, text_ref), (image_gain_hbm, image_gain_ref),
            (text_gain_hbm, text_gain_ref), (scale_hbm, scale_ref), (pair_hbm, pair_ref),
        ])
    ]
    for copy in small[:4]:
        copy.start()

    @pl.when(module == 0)
    def _():
        text_copy.start()
        image_copy.start()

    @pl.when(module != 0)
    def _():
        image_copy.start()
        text_copy.start()

    for copy in small[4:]:
        copy.start()
    for copy in small:
        copy.wait()

    def embed(pooled_ref, gain_ref, copy, w):
        features = pooled_ref[...].astype(jnp.float32)
        centered = features - jnp.mean(features, axis=-1, keepdims=True)
        variance = jnp.mean(centered * centered, axis=-1, keepdims=True)
        normed = centered * lax.rsqrt(variance + 1e-05) * gain_ref[...].reshape(1, -1)
        normed = normed.astype(jnp.bfloat16)
        copy.wait()
        embedded = jnp.dot(normed, w[...], preferred_element_type=jnp.float32)
        lengths = jnp.sqrt(jnp.sum(embedded * embedded, axis=-1, keepdims=True) + 1e-06)
        return embedded / lengths, lengths

    depth = rows_all.shape[-1]

    def embed_other(*args):
        rows = embed(*args)[0].astype(jnp.bfloat16)
        for h in range(CHUNKS):
            rows_all[me, h] = rows[:, h * depth : (h + 1) * depth]

    def embed_own(*args):
        unit[...], length[...] = embed(*args)

    image_args = (image_ref, image_gain_ref, image_copy, image_w)
    text_args = (text_ref, text_gain_ref, text_copy, text_w)

    pl.when(module == 0)(lambda: embed_other(*text_args))
    pl.when(module != 0)(lambda: embed_other(*image_args))

    pl.semaphore_wait(barrier, n_line + 2)

    def send(block, h, target, sem):
        return pltpu.make_async_remote_copy(
            src_ref=rows_all.at[block, h], dst_ref=rows_all.at[block, h],
            send_sem=send_sem.at[sem, h], recv_sem=recv_sem.at[block, h],
            device_id=(module, target), device_id_type=MESH,
        )

    def line_send(step, h):
        return send(me, h, peer(by_distance(line, n_line, step, True), side, core), step)

    def across_send(q, h, step):
        return send(peer(q, side, core), h, across, n_line + step)

    def twin_send(q, b, h, step):
        return send(peer(q, b, core), h, twin, n_line * 2 + step)

    for h in range(CHUNKS):
        across_send(line, h, 0).start()
        loop(n_line - 1, lambda step: line_send(step, h).start())
        twin_send(line, side, h, 0).start()

    pl.when(module == 0)(lambda: embed_own(*image_args))
    pl.when(module != 0)(lambda: embed_own(*text_args))
    own_half = unit[...].astype(jnp.bfloat16)
    scale_value = scale_ref[0]

    def score(block):
        products = 0.0
        for h in range(CHUNKS):
            products = products + lax.dot_general(
                own_half[:, h * depth : (h + 1) * depth], rows_all[block, h],
                (((1,), (1,)), ((), ())), preferred_element_type=jnp.float32,
            )
        scores[block] = scale_value * products

    def arrive(block, h):
        send(block, h, twin, 0).wait_recv()

    score(me)

    for h in range(CHUNKS):
        arrive(across, h)
        twin_send(line, 1 - side, h, n_line).start()
    score(across)

    def from_line(step):
        q = by_distance(line, n_line, step, False)
        for h in range(CHUNKS):
            arrive(peer(q, side, core), h)
            across_send(q, h, step + 1).start()
            twin_send(q, side, h, step + 1).start()
        score(peer(q, side, core))

    def from_across(step):
        q = by_distance(line, n_line, step, False)
        for h in range(CHUNKS):
            arrive(peer(q, 1 - side, core), h)
            twin_send(q, 1 - side, h, n_line + step + 1).start()
        score(peer(q, 1 - side, core))

    def from_twin(b, q):
        block = peer(q, b, 1 - core)
        for h in range(CHUNKS):
            arrive(block, h)
        score(block)

    from_twin(side, line)
    from_twin(1 - side, line)
    loop(n_line - 1, from_line)
    loop(n_line - 1, lambda step: from_twin(side, by_distance(line, n_line, step, False)))
    loop(n_line - 1, from_across)
    loop(n_line - 1, lambda step: from_twin(1 - side, by_distance(line, n_line, step, False)))
    pl.semaphore_signal(ready, inc=1, device_id=(mirror, me), device_id_type=MESH)

    square = (row_count, row_count)
    down = lax.broadcasted_iota(jnp.int32, square, 0)
    over = lax.broadcasted_iota(jnp.int32, square, 1)
    pairs = jnp.sum(
        jnp.where(down == over, pair_ref[...].astype(jnp.float32), 0.0), axis=1, keepdims=True
    ).astype(jnp.int32)

    def matched(block):
        return over + block * row_count == pairs

    peak = fold(n_dp, lambda p, acc: jnp.maximum(acc, scores[p]), jnp.full(square, -jnp.inf, jnp.float32))
    peak = jnp.max(peak, axis=1, keepdims=True)

    def gather_sums(p, acc):
        total, diagonal = acc
        block = scores[p]
        return total + jnp.exp(block - peak), diagonal + jnp.where(matched(p), block, 0.0)

    zero = jnp.zeros(square, jnp.float32)
    total, diagonal = fold(n_dp, gather_sums, (zero, zero))
    lse = peak + jnp.log(jnp.sum(total, axis=1, keepdims=True))
    excess = lse - jnp.sum(diagonal, axis=1, keepdims=True)

    lanes = note.shape[-1]
    wide = (row_count, lanes)
    lane = lax.broadcasted_iota(jnp.int32, wide, 1)
    placed = jnp.where(
        lane == lax.broadcasted_iota(jnp.int32, wide, 0), lse, jnp.where(lane == lanes - 1, excess, 0.0)
    )
    note[...] = jnp.sum(placed, axis=0, keepdims=True)
    notes[here] = note[...]

    def mirror_target(step):
        if n_line > 8:
            return (me + step) % n_dp
        q = by_distance(line, n_line, step // 4, True) if step // 4 < n_line - 1 else line
        return q * 4 + step % 4

    def note_copy(target_module, target, slot, step):
        return pltpu.make_async_remote_copy(
            src_ref=note, dst_ref=notes.at[slot],
            send_sem=note_send.at[step], recv_sem=note_recv.at[slot],
            device_id=(target_module, target), device_id_type=MESH,
        )

    def mirror_note(step):
        return note_copy(mirror, mirror_target(step), here, step)

    def same_note(step):
        return note_copy(module, (me + 1 + step) % n_dp, here, n_dp + step)

    pl.semaphore_wait(ready, 1)
    loop(n_dp, lambda step: mirror_note(step).start())
    loop(n_dp - 1, lambda step: same_note(step).start())

    def first_half(p):
        base[p] = jnp.exp(scores[p] - lse) - jnp.where(matched(p), 2.0, 0.0)

    loop(n_dp, first_half)

    loop(n_dp, lambda step: note_copy(mirror, step, mirror * n_dp + step, step).wait_recv())

    def weigh(p, acc):
        other = notes[mirror * n_dp + p][:, :row_count]
        weight = (base[p] + jnp.exp(scores[p] - other)).astype(jnp.bfloat16)
        return tuple(
            acc[h] + jnp.dot(weight, rows_all[p, h], preferred_element_type=jnp.float32)
            for h in range(CHUNKS)
        )

    zeros = tuple(jnp.zeros((row_count, depth), jnp.float32) for _ in range(CHUNKS))
    moved = scale_value * jnp.concatenate(fold(n_dp, weigh, zeros), axis=1)
    own = unit[...]
    grad_ref[0] = (moved - own * jnp.sum(own * moved, axis=-1, keepdims=True)) / length[...]

    def same_arrive(step):
        other = (me + 1 + step) % n_dp
        note_copy(module, other, module * n_dp + other, n_dp + step).wait_recv()

    loop(n_dp - 1, same_arrive)
    loss = fold(n_all, lambda p, acc: acc + notes[p], jnp.zeros((1, lanes), jnp.float32))
    loss_ref[...] = loss[:, lanes - 1 :]

    for h in range(CHUNKS):
        loop(n_line - 1, lambda step: line_send(step, h).wait_send())
        loop(n_line, lambda step: across_send(line, h, step).wait_send())
        loop(2 * n_line, lambda step: twin_send(line, side, h, step).wait_send())
    loop(n_dp, lambda step: mirror_note(step).wait_send())
    loop(n_dp - 1, lambda step: same_note(step).wait_send())


def solution(mesh):
    n_mod, n_dp = mesh.shape["mod"], mesh.shape["dp"]

    def local(
        image_pooled, text_pooled, image_gain, text_gain, image_proj, text_proj, logit_scale, pair_index
    ):
        rows = image_pooled.shape[0]
        width = image_proj.shape[1]
        lanes = -(-(rows + 1) // 128) * 128
        n_all = n_mod * n_dp
        vmem = pl.BlockSpec(memory_space=pltpu.VMEM)
        dma = pltpu.SemaphoreType.DMA
        loss, grad = pl.pallas_call(
            functools.partial(kernel, n_mod, n_dp),
            out_shape=(
                jax.ShapeDtypeStruct((1, 1), jnp.float32),
                jax.ShapeDtypeStruct((1, rows, width), jnp.float32),
            ),
            in_specs=[pl.BlockSpec(memory_space=pltpu.HBM)] * 8,
            out_specs=(vmem, vmem),
            scratch_shapes=[
                pltpu.VMEM(image_pooled.shape, image_pooled.dtype),
                pltpu.VMEM(text_pooled.shape, text_pooled.dtype),
                pltpu.VMEM(image_gain.shape, jnp.float32),
                pltpu.VMEM(text_gain.shape, jnp.float32),
                pltpu.SMEM((1,), jnp.float32),
                pltpu.VMEM(pair_index.shape, pair_index.dtype),
                pltpu.VMEM(image_proj.shape, image_proj.dtype),
                pltpu.VMEM(text_proj.shape, text_proj.dtype),
                pltpu.VMEM((n_dp, CHUNKS, rows, width // CHUNKS), jnp.bfloat16),
                pltpu.VMEM((rows, width), jnp.float32),
                pltpu.VMEM((rows, 1), jnp.float32),
                pltpu.VMEM((n_dp, rows, rows), jnp.float32),
                pltpu.VMEM((n_dp, rows, rows), jnp.float32),
                pltpu.VMEM((1, lanes), jnp.float32),
                pltpu.VMEM((n_all, 1, lanes), jnp.float32),
                dma((6,)),
                dma((2,)),
                dma((n_dp, CHUNKS)),
                dma((n_dp, CHUNKS)),
                dma((n_all,)),
                dma((n_all,)),
                pltpu.SemaphoreType.REGULAR,
            ],
            compiler_params=pltpu.CompilerParams(collective_id=0, has_side_effects=True),
        )(image_pooled, text_pooled, image_gain, text_gain, image_proj, text_proj, logit_scale, pair_index)
        batch_total = 2.0 * n_dp * rows
        return loss[0, 0] / batch_total, grad / batch_total

    in_specs = (P("dp", None), P("dp", None), P(), P(), P(), P(), P(), P("mod", "dp"))
    out_specs = (P(), P("mod", "dp", None))
    return jax.shard_map(local, mesh=mesh, in_specs=in_specs, out_specs=out_specs, check_vma=False)
```

time: 33.1 us -> 30 us (0.906)
  Pallas kernels: 28.2 us -> 25.1 us
  other arithmetic: 0 us -> 1.56 us
  local copies, waits for them, and re-layouts: 1.56 us -> 0 us
    pallas_call x1, Pallas kernels: 28.2 us -> 25.1 us  [local(): pl.pallas_call(functools.partial(kernel, n_mod, n_dp), out_shape=(jax.Sha...]
    div x0 -> x1, other arithmetic: none -> 1.56 us  [local(): return (loss[0, 0] / batch_total, grad / batch_total)]
    unnamed x1 -> x0, local copies, waits for them, and re-layouts: 1.56 us -> none
where the time goes in v2:
time: 30 us; the launch traced here: 29.8 us
  Pallas kernels  25.1 us (84%)
  between operations  3.1 us (10%)
  other arithmetic  1.56 us (5%)
    pallas_call x1, Pallas kernels, local(): pl.pallas_call(functools.partial(kernel, n_mod, n_dp), out_shape=(jax.Sha...  25.1 us
    div x1, other arithmetic, local(): return (loss[0, 0] / batch_total, grad / batch_total)  1.56 us

profile of v2, /device:TPU:0, one launch (start us, length us, event | category | flops | bytes accessed | tf_op | source)
XLA Modules:
  0.0 29.8 jit_solution(9259640899193016699)
XLA Ops:
  1.3 25.1 %shard_map.95 = (f32[1,1]{1,0:T(1,128)}, f32[1,40,768]{2,1,0:T(8,128)}) custom-call(bf16[40,1024]{1,0:T(8,128)(2,1)} %image_hbm.1, bf16[40,768]{1,0:T(8,128)(2,1)} %text_hbm.1, f32[1024]{0:T(1024)} %image_gain_hbm.1, f32[768]{0:T(1024)} %text_gain_hbm.1, bf16[1024,768]{1,0:T(8,128)(2,1)} %image_proj_ref.1, bf16[768,768]{1,0:T(8,128)(2,1)} %text_proj_ref.1, ...), custom_call_target="tpu_custom_call" | custom-call | tf_op jit(solution)/shard_map/pallas_call | solution.py:312
  27.1 1.6 %broadcast_multiply_fusion = f32[1,40,768]{2,1,0:T(8,128)} fusion(f32[1,40,768]{2,1,0:T(8,128)} %get-tuple-element.5), kind=kLoop, calls=%fused_computation | loop fusion | flops 30720 | bytes 245760 | tf_op jit(solution)/shard_map/div | solution.py:347

commit v3 on v2

--- a/solution.py
+++ b/solution.py
@@ -10,6 +10,7 @@
 MESH = pl.DeviceIdType.MESH
 UNROLL = 32
 CHUNKS = 2
+SLICES = 1
 
 
 def pick(index, values):
@@ -47,9 +48,9 @@
 
 def kernel(
     n_mod, n_dp,
-    image_hbm, text_hbm, image_gain_hbm, text_gain_hbm, image_proj_ref, text_proj_ref, scale_hbm, pair_hbm,
+    image_hbm, text_hbm, image_gain_hbm, text_gain_hbm, image_proj_ref, text_proj_ref, scale_ref, pair_hbm,
     loss_ref, grad_ref,
-    image_ref, text_ref, image_gain_ref, text_gain_ref, scale_ref, pair_ref,
+    image_ref, text_ref, image_gain_ref, text_gain_ref, pair_ref,
     image_w, text_w, rows_all, unit, length, scores, base, note, notes,
     in_sem, w_sem, send_sem, recv_sem, note_send, note_recv, ready,
 ):
@@ -76,13 +77,26 @@
     greet(module, twin)
     greet(mirror, me)
 
-    image_copy = pltpu.make_async_copy(image_proj_ref, image_w, w_sem.at[0])
-    text_copy = pltpu.make_async_copy(text_proj_ref, text_w, w_sem.at[1])
+    def slices(source, target, at):
+        tall = source.shape[0] // SLICES
+        return [
+            pltpu.make_async_copy(
+                source.at[pl.ds(k * tall, tall)], target.at[pl.ds(k * tall, tall)], w_sem.at[at, k]
+            )
+            for k in range(SLICES)
+        ]
+
+    image_copy, text_copy = slices(image_proj_ref, image_w, 0), slices(text_proj_ref, text_w, 1)
+
+    def start(copies):
+        for copy in copies:
+            copy.start()
+
     small = [
         pltpu.make_async_copy(source, target, in_sem.at[at])
         for at, (source, target) in enumerate([
             (image_hbm, image_ref), (text_hbm, text_ref), (image_gain_hbm, image_gain_ref),
-            (text_gain_hbm, text_gain_ref), (scale_hbm, scale_ref), (pair_hbm, pair_ref),
+            (text_gain_hbm, text_gain_ref), (pair_hbm, pair_ref),
         ])
     ]
     for copy in small[:4]:
@@ -90,27 +104,33 @@
 
     @pl.when(module == 0)
     def _():
-        text_copy.start()
-        image_copy.start()
+        start(text_copy)
+        start(image_copy)
 
     @pl.when(module != 0)
     def _():
-        image_copy.start()
-        text_copy.start()
+        start(image_copy)
+        start(text_copy)
 
     for copy in small[4:]:
         copy.start()
     for copy in small:
         copy.wait()
 
-    def embed(pooled_ref, gain_ref, copy, w):
+    def embed(pooled_ref, gain_ref, copies, w):
         features = pooled_ref[...].astype(jnp.float32)
         centered = features - jnp.mean(features, axis=-1, keepdims=True)
         variance = jnp.mean(centered * centered, axis=-1, keepdims=True)
         normed = centered * lax.rsqrt(variance + 1e-05) * gain_ref[...].reshape(1, -1)
         normed = normed.astype(jnp.bfloat16)
-        copy.wait()
-        embedded = jnp.dot(normed, w[...], preferred_element_type=jnp.float32)
+        tall = w.shape[0] // SLICES
+        embedded = 0.0
+        for k in range(SLICES):
+            copies[k].wait()
+            embedded = embedded + jnp.dot(
+                normed[:, k * tall : (k + 1) * tall], w[k * tall : (k + 1) * tall],
+                preferred_element_type=jnp.float32,
+            )
         lengths = jnp.sqrt(jnp.sum(embedded * embedded, axis=-1, keepdims=True) + 1e-06)
         return embedded / lengths, lengths
 
@@ -156,7 +176,7 @@
     pl.when(module == 0)(lambda: embed_own(*image_args))
     pl.when(module != 0)(lambda: embed_own(*text_args))
     own_half = unit[...].astype(jnp.bfloat16)
-    scale_value = scale_ref[0]
+    scale_value = scale_ref[...].reshape(1, 1)
 
     def score(block):
         products = 0.0
@@ -312,17 +332,17 @@
         loss, grad = pl.pallas_call(
             functools.partial(kernel, n_mod, n_dp),
             out_shape=(
-                jax.ShapeDtypeStruct((1, 1), jnp.float32),
-                jax.ShapeDtypeStruct((1, rows, width), jnp.float32),
+                pltpu.VMEM((1, 1), jnp.float32),
+                pltpu.VMEM((1, rows, width), jnp.float32),
             ),
-            in_specs=[pl.BlockSpec(memory_space=pltpu.HBM)] * 8,
+            in_specs=[pl.BlockSpec(memory_space=pltpu.HBM)] * 6
+            + [vmem, pl.BlockSpec(memory_space=pltpu.HBM)],
             out_specs=(vmem, vmem),
             scratch_shapes=[
                 pltpu.VMEM(image_pooled.shape, image_pooled.dtype),
                 pltpu.VMEM(text_pooled.shape, text_pooled.dtype),
                 pltpu.VMEM(image_gain.shape, jnp.float32),
                 pltpu.VMEM(text_gain.shape, jnp.float32),
-                pltpu.SMEM((1,), jnp.float32),
                 pltpu.VMEM(pair_index.shape, pair_index.dtype),
                 pltpu.VMEM(image_proj.shape, image_proj.dtype),
                 pltpu.VMEM(text_proj.shape, text_proj.dtype),
@@ -333,8 +353,8 @@
                 pltpu.VMEM((n_dp, rows, rows), jnp.float32),
                 pltpu.VMEM((1, lanes), jnp.float32),
                 pltpu.VMEM((n_all, 1, lanes), jnp.float32),
-                dma((6,)),
-                dma((2,)),
+                dma((5,)),
+                dma((2, SLICES)),
                 dma((n_dp, CHUNKS)),
                 dma((n_dp, CHUNKS)),
                 dma((n_all,)),

time: 30 us -> 28.9 us (0.963)
  other arithmetic: 1.56 us -> 0.66 us
    div x1, other arithmetic: 1.56 us -> 0.66 us  [local(): return (loss[0, 0] / batch_total, grad / batch_total)]
where the time goes in v3:
time: 28.9 us; the launch traced here: 28.7 us
  Pallas kernels  25.1 us (87%)
  between operations  2.98 us (10%)
  other arithmetic  0.66 us (2%)
    pallas_call x1, Pallas kernels, local(): pl.pallas_call(functools.partial(kernel, n_mod, n_dp), out_shape=(pltpu.V...  25.1 us
    div x1, other arithmetic, local(): return (loss[0, 0] / batch_total, grad / batch_total)  0.66 us

profile of v3, /device:TPU:0, one launch (start us, length us, event | category | flops | bytes accessed | tf_op | source)
XLA Modules:
  0.0 28.7 jit_solution(6330280492503916040)
XLA Ops:
  1.3 25.1 %shard_map.95 = (f32[1,1]{1,0:T(1,128)}, f32[1,40,768]{2,1,0:T(8,128)S(1)}) custom-call(bf16[40,1024]{1,0:T(8,128)(2,1)} %image_hbm.1, bf16[40,768]{1,0:T(8,128)(2,1)} %text_hbm.1, f32[1024]{0:T(1024)} %image_gain_hbm.1, f32[768]{0:T(1024)} %text_gain_hbm.1, bf16[1024,768]{1,0:T(8,128)(2,1)} %image_proj_ref.1, bf16[768,768]{1,0:T(8,128)(2,1)} %text_proj_ref.1, ...), custom_call_target="tpu_custom_call" | custom-call | tf_op jit(solution)/shard_map/pallas_call | solution.py:332
  26.9 0.7 %broadcast_multiply_fusion = f32[1,40,768]{2,1,0:T(8,128)} fusion(f32[1,40,768]{2,1,0:T(8,128)S(1)} %get-tuple-element.5), kind=kLoop, calls=%fused_computation | loop fusion | flops 30720 | bytes 245760 | tf_op jit(solution)/shard_map/div | solution.py:367
